TPU v7x, 32 devices: a whole 2x2x4 slice. The times are simulated.
32 devices in a mesh: dp: 4 (over z), row: 2 (over x), col: 4 (over y, core).
Axes of the slice: x: 2, y: 2, z: 4, core: 2. Of those that a mesh axis runs over, the one named last changes fastest.
Arguments:
- block_input: bfloat16 [8192, 1536], P('dp', 'row'), may hold values from -16 to 16
- positions: int32 [8192], P('dp'), may hold values from 0 to 511, as said below
- attn_gain: float32 [1536], P('row'), may hold values from 0.5 to 1.5
- w_qkv: bfloat16 [1536, 3072], P('row', 'col'), may hold values from -1.04613624 to 1.04613624
- w_out: bfloat16 [1536, 1536], P('col', 'row'), may hold values from -1.25 to 1.25
- ffn_gain: float32 [1536], P('row'), may hold values from 0.5 to 1.5
- w_gate: bfloat16 [1536, 4096], P('row', 'col'), may hold values from -0.15625 to 0.15625
- w_up: bfloat16 [1536, 4096], P('row', 'col'), may hold values from -0.15625 to 0.15625
- w_down: bfloat16 [4096, 1536], P('col', 'row'), may hold values from -0.09375 to 0.09375
- out_grad: bfloat16 [8192, 1536], P('dp', 'row'), may hold values from -6 to 6
Outputs:
- block_output: bfloat16 [8192, 1536], P('dp', 'row')
- input_grad: bfloat16 [8192, 1536], P('dp', 'row')
- attn_gain_grad: float32 [1536], P('row')
- w_qkv_grad: float32 [1536, 3072], P('row', 'col')
- w_out_grad: float32 [1536, 1536], P('col', 'row')
- ffn_gain_grad: float32 [1536], P('row')
- w_gate_grad: float32 [1536, 4096], P('row', 'col')
- w_up_grad: float32 [1536, 4096], P('row', 'col')
- w_down_grad: float32 [4096, 1536], P('col', 'row')
Inputs may be any that keep to these rules, and one draw needn't show every extreme that they name: `positions`: each sequence of 512 tokens holds one to five packed documents; a token's position counts from the first token of its document; some sequence is a single document.
All inputs are finite; a program needn't handle non-finite values.
Results may differ from a plain program's by a relative error of at most 0.015.
Values may be sent and summed in bfloat16 or wider, within the bound.
A program may use at most 192 MiB of HBM per device.

v0:
```python
import jax
import jax.numpy as jnp
from jax import lax
from jax.sharding import PartitionSpec as P

D = 1536
H = 16
KV = 8
HD = 96
SEQ_LEN = 512
EPS = 1e-05
THETA = 100000.0


def rotate(values, cosine, sine, sign):
    half = values.shape[-1] // 2
    first = values[..., :half]
    second = values[..., half:]
    return jnp.concatenate(
        [first * cosine - sign * second * sine, second * cosine + sign * first * sine], axis=-1
    )


def angle_tables(pos):
    freqs = THETA ** (-(jnp.arange(0, HD, 2).astype(jnp.float32) / HD))
    angles = pos.astype(jnp.float32)[..., None] * freqs
    return (jnp.cos(angles), jnp.sin(angles))


def norm_stat(values):
    return lax.psum(values, "row")


def width_total(values):
    return lax.psum(values, "col")


def join_rows(values):
    return lax.all_gather(values, "row", axis=0, tiled=True)


def split_rows(left, right, contract):
    return lax.psum_scatter(
        lax.dot_general(
            left, right, (((1,), (contract,)), ((), ())), preferred_element_type=jnp.float32
        ),
        "row",
        scatter_dimension=0,
        tiled=True,
    )


def left_product(left, right):
    return lax.dot_general(
        left, right, (((0,), (0,)), ((), ())), preferred_element_type=jnp.float32
    )


def right_product(left, right):
    return lax.dot_general(
        left, right, (((1,), (1,)), ((), ())), preferred_element_type=jnp.float32
    )


def swiglu_back(gate, up, grad):
    sig = jax.nn.sigmoid(gate)
    gate_grad = (grad * up * sig * (1.0 + gate * (1.0 - sig))).astype(jnp.bfloat16)
    up_grad = (grad * gate * sig).astype(jnp.bfloat16)
    return (gate_grad, up_grad)


def body(block_input, positions, attn_gain, w_qkv, w_out, ffn_gain, w_gate, w_up, w_down, out_grad):
    f32 = jnp.float32
    bf = jnp.bfloat16
    rows_all = block_input.shape[0]
    rows_half = rows_all // lax.axis_size("row")
    group = H // KV
    kv_local = w_qkv.shape[1] // ((group + 2) * HD)
    seqs_local = rows_half // SEQ_LEN
    scale = HD ** (-0.5)
    xf = block_input.astype(f32)
    inv1 = lax.rsqrt(norm_stat(jnp.sum(xf * xf, axis=1, keepdims=True)) / D + EPS)
    normed1 = (xf * inv1 * attn_gain).astype(bf)
    qkv_half = split_rows(normed1, w_qkv, 0)
    grouped = qkv_half.reshape(seqs_local, SEQ_LEN, kv_local, group + 2, HD)
    pos_half = lax.dynamic_slice_in_dim(
        positions, lax.axis_index("row") * rows_half, rows_half
    ).reshape(seqs_local, SEQ_LEN)
    cosine, sine = angle_tables(pos_half)
    cq = cosine[:, :, None, None, :]
    sq = sine[:, :, None, None, :]
    ck = cosine[:, :, None, :]
    sk = sine[:, :, None, :]
    queries = rotate(grouped[:, :, :, :group], cq, sq, 1.0).astype(bf)
    keys = rotate(grouped[:, :, :, group], ck, sk, 1.0).astype(bf)
    vals = grouped[:, :, :, group + 1].astype(bf)
    causal = jnp.arange(SEQ_LEN)[:, None] >= jnp.arange(SEQ_LEN)[None, :]
    scores = jnp.einsum("sikph,sjkh->skpij", queries, keys, preferred_element_type=f32) * scale
    scores = jnp.where(causal, scores, -1e30)
    top = jnp.max(scores, axis=-1, keepdims=True)
    lse = top + jnp.log(jnp.sum(jnp.exp(scores - top), axis=-1, keepdims=True))
    probs_b = jnp.exp(scores - lse).astype(bf)
    mixed = jnp.einsum("skpij,sjkh->sikph", probs_b, vals, preferred_element_type=f32).astype(bf)
    attn_rows = join_rows(mixed.reshape(rows_half, kv_local * group * HD))
    hidden = xf + width_total(jnp.dot(attn_rows, w_out, preferred_element_type=f32))
    inv2 = lax.rsqrt(norm_stat(jnp.sum(hidden * hidden, axis=1, keepdims=True)) / D + EPS)
    normed2 = (hidden * inv2 * ffn_gain).astype(bf)
    gate_part = jnp.dot(normed2, w_gate, preferred_element_type=f32)
    up_part = jnp.dot(normed2, w_up, preferred_element_type=f32)
    gate_kept, up_kept = (
        lax.psum_scatter(gate_part, "row", scatter_dimension=0, tiled=True),
        lax.psum_scatter(up_part, "row", scatter_dimension=0, tiled=True),
    )
    act_half = (jax.nn.silu(gate_kept) * up_kept).astype(bf)
    act_rows = lax.all_gather(act_half, "row", axis=0, tiled=True)
    block_output = (
        hidden + width_total(jnp.dot(act_rows, w_down, preferred_element_type=f32))
    ).astype(bf)
    w_down_grad = left_product(act_rows, out_grad)
    act_grad_part = right_product(out_grad, w_down)
    act_grad_half = lax.psum_scatter(act_grad_part, "row", scatter_dimension=0, tiled=True)
    gate_half, up_half = swiglu_back(gate_kept, up_kept, act_grad_half)
    gate_grad, up_grad = (
        lax.all_gather(gate_half, "row", axis=0, tiled=True),
        lax.all_gather(up_half, "row", axis=0, tiled=True),
    )
    w_gate_grad = left_product(normed2, gate_grad)
    w_up_grad = left_product(normed2, up_grad)
    normed2_grad = width_total(right_product(gate_grad, w_gate) + right_product(up_grad, w_up))
    ffn_gain_grad = jnp.sum(normed2_grad * hidden * inv2, axis=0)
    scaled2 = normed2_grad * ffn_gain
    hidden_grad = out_grad.astype(f32) + inv2 * (
        scaled2
        - hidden * inv2 * inv2 * norm_stat(jnp.sum(scaled2 * hidden, axis=1, keepdims=True)) / D
    )
    hidden_b = hidden_grad.astype(bf)
    w_out_grad = left_product(attn_rows, hidden_b)
    mixed_grad = (
        split_rows(hidden_b, w_out, 1).astype(bf).reshape(seqs_local, SEQ_LEN, kv_local, group, HD)
    )
    probs = jnp.exp(scores - lse)
    value_grad = jnp.einsum("skpij,sikph->sjkh", probs_b, mixed_grad, preferred_element_type=f32)
    prob_grad = jnp.einsum("sikph,sjkh->skpij", mixed_grad, vals, preferred_element_type=f32)
    delta = jnp.sum(mixed_grad.astype(f32) * mixed.astype(f32), axis=-1)
    delta = jnp.transpose(delta, (0, 2, 3, 1))[..., None]
    score_grad = (probs * (prob_grad - delta)).astype(bf)
    query_grad = rotate(
        jnp.einsum("skpij,sjkh->sikph", score_grad, keys, preferred_element_type=f32) * scale,
        cq,
        sq,
        -1.0,
    )
    key_grad = rotate(
        jnp.einsum("skpij,sikph->sjkh", score_grad, queries, preferred_element_type=f32) * scale,
        ck,
        sk,
        -1.0,
    )
    packed = jnp.concatenate(
        [query_grad, key_grad[:, :, :, None], value_grad[:, :, :, None]], axis=3
    ).astype(bf)
    qkv_grad = join_rows(packed.reshape(rows_half, w_qkv.shape[1]))
    w_qkv_grad = left_product(normed1, qkv_grad)
    normed1_grad = width_total(right_product(qkv_grad, w_qkv))
    attn_gain_grad = jnp.sum(normed1_grad * xf * inv1, axis=0)
    scaled1 = normed1_grad * attn_gain
    input_grad = (
        hidden_grad
        + inv1
        * (scaled1 - xf * inv1 * inv1 * norm_stat(jnp.sum(scaled1 * xf, axis=1, keepdims=True)) / D)
    ).astype(bf)
    attn_gain_grad, w_qkv_grad, w_out_grad, ffn_gain_grad, w_gate_grad, w_up_grad, w_down_grad = (
        lax.psum(attn_gain_grad.astype(jnp.bfloat16), "dp").astype(jnp.float32),
        lax.psum(w_qkv_grad.astype(jnp.bfloat16), "dp").astype(jnp.float32),
        lax.psum(w_out_grad.astype(jnp.bfloat16), "dp").astype(jnp.float32),
        lax.psum(ffn_gain_grad.astype(jnp.bfloat16), "dp").astype(jnp.float32),
        lax.psum(w_gate_grad.astype(jnp.bfloat16), "dp").astype(jnp.float32),
        lax.psum(w_up_grad.astype(jnp.bfloat16), "dp").astype(jnp.float32),
        lax.psum(w_down_grad.astype(jnp.bfloat16), "dp").astype(jnp.float32),
    )
    return (
        block_output,
        input_grad,
        attn_gain_grad,
        w_qkv_grad,
        w_out_grad,
        ffn_gain_grad,
        w_gate_grad,
        w_up_grad,
        w_down_grad,
    )


def solution(mesh):
    return jax.shard_map(
        body,
        mesh=mesh,
        in_specs=(
            P("dp", "row"),
            P("dp"),
            P("row"),
            P("row", "col"),
            P("col", "row"),
            P("row"),
            P("row", "col"),
            P("row", "col"),
            P("col", "row"),
            P("dp", "row"),
        ),
        out_specs=(
            P("dp", "row"),
            P("dp", "row"),
            P("row"),
            P("row", "col"),
            P("col", "row"),
            P("row"),
            P("row", "col"),
            P("row", "col"),
            P("col", "row"),
        ),
        check_vma=False,
    )
```

profile of v0, /device:TPU:0, one launch (start us, length us, event | category | flops | bytes accessed | tf_op | source)
XLA Modules:
  0.0 1491.3 jit_solution(6194909048291860447)
XLA Ops:
  7.2 2.7 fusion.12
  9.9 5.9 psum.105
  15.9 7.6 fusion.30
  25.0 77.5 %reduce-scatter.6.cloned.1.call-done = f32[1024,768]{1,0:T(8,128)} async-done(((f32[2048,768]{1,0:T(8,128)}), f32[1024,768]{1,0:T(8,128)}) %reduce-scatter.6.cloned.1.call-update) | async-done | bytes 3145744 | tf_op jit(solution)/shard_map/reduce_scatter | solution.py:43
  102.6 3.5 copy.27
  106.1 5.6 reshape.64
  121.5 3.3 fusion.24
  126.9 27.1 %all-gather.6.cloned.1.call-done = bf16[2048,384]{0,1:T(8,128)(2,1)} async-done(((bf16[1024,384]{0,1:T(8,128)(2,1)}), bf16[2048,384]{0,1:T(8,128)(2,1)}) %all-gather.6.cloned.1.call-update) | async-done | bytes 1572880 | tf_op jit(solution)/shard_map/all_gather | solution.py:39
  154.0 6.0 fusion.42
  160.1 9.1 fusion.46
  169.3 110.5 %all-reduce.8.cloned.1.call-done = f32[2048,768]{1,0:T(8,128)} async-done(((f32[2048,768]{1,0:T(8,128)}), f32[2048,768]{1,0:T(8,128)}) %all-reduce.8.cloned.1.call-update) | async-done | bytes 6291472 | tf_op jit(solution)/shard_map/psum | solution.py:35
  279.8 7.2 multiply_reduce_fusion.2
  287.0 5.2 psum.107
  292.2 3.5 multiply_convert_fusion
  297.4 5.6 fusion.44
  303.1 7.6 fusion.43
  310.8 70.9 %reduce-scatter.12.cloned.1.call-done = f32[1024,1024]{1,0:T(8,128)} async-done(((f32[2048,1024]{1,0:T(8,128)}), f32[1024,1024]{1,0:T(8,128)}) %reduce-scatter.12.cloned.1.call-update) | async-done | bytes 4194320 | tf_op jit(solution)/shard_map/reduce_scatter | solution.py:121
  381.7 101.5 %reduce-scatter.10.cloned.1.call-done = f32[1024,1024]{1,0:T(8,128)} async-done(((f32[2048,1024]{1,0:T(8,128)}), f32[1024,1024]{1,0:T(8,128)}) %reduce-scatter.10.cloned.1.call-update) | async-done | bytes 4194320 | tf_op jit(solution)/shard_map/reduce_scatter | solution.py:112
  483.2 101.5 %reduce-scatter.8.cloned.1.call-done = f32[1024,1024]{1,0:T(8,128)} async-done(((f32[2048,1024]{1,0:T(8,128)}), f32[1024,1024]{1,0:T(8,128)}) %reduce-scatter.8.cloned.1.call-update) | async-done | bytes 4194320 | tf_op jit(solution)/shard_map/reduce_scatter | solution.py:111
  584.7 8.1 multiply_convert_fusion.1
  594.1 55.6 %all-gather.10.cloned.1.call-done = bf16[2048,1024]{1,0:T(8,128)(2,1)} async-done(((bf16[1024,1024]{1,0:T(8,128)(2,1)}), bf16[2048,1024]{1,0:T(8,128)(2,1)}) %all-gather.10.cloned.1.call-update) | async-done | bytes 4194320 | tf_op jit(solution)/shard_map/all_gather | solution.py:124
  649.7 8.3 fusion.47
  658.0 50.6 %all-gather.12.cloned.1.call-done = bf16[2048,1024]{1,0:T(8,128)(2,1)} async-done(((bf16[1024,1024]{1,0:T(8,128)(2,1)}), bf16[2048,1024]{1,0:T(8,128)(2,1)}) %all-gather.12.cloned.1.call-update) | async-done | bytes 4194320 | tf_op jit(solution)/shard_map/all_gather | solution.py:125
  708.6 10.6 convolution_add_fusion
  719.3 119.7 %all-reduce.10.cloned.1.call-done = f32[2048,768]{1,0:T(8,128)} async-done(((f32[2048,768]{1,0:T(8,128)}), f32[2048,768]{1,0:T(8,128)}) %all-reduce.10.cloned.1.call-update) | async-done | bytes 6291472 | tf_op jit(solution)/shard_map/psum | solution.py:35
  839.0 5.4 multiply_reduce_fusion
  844.4 5.0 psum.110
  849.4 6.7 multiply_add_fusion
  856.1 2.6 copy-done.2
  858.7 3.5 fusion.19
  863.2 42.8 %reduce-scatter.14.cloned.1.call-done = f32[1024,384]{1,0:T(8,128)} async-done(((f32[2048,384]{1,0:T(8,128)}), f32[1024,384]{1,0:T(8,128)}) %reduce-scatter.14.cloned.1.call-update) | async-done | bytes 1572880 | tf_op jit(solution)/shard_map/reduce_scatter | solution.py:43
  909.8 5.3 fusion.1
  925.8 39.1 %all-gather.8.cloned.1.call-done = bf16[2048,1024]{1,0:T(8,128)(2,1)} async-done(((bf16[1024,1024]{1,0:T(8,128)(2,1)}), bf16[2048,1024]{1,0:T(8,128)(2,1)}) %all-gather.8.cloned.1.call-update) | async-done | bytes 4194320 | tf_op jit(solution)/shard_map/all_gather | solution.py:115
  964.9 8.2 fusion.45
  973.1 38.7 %all-gather.14.cloned.1.call-done = bf16[2048,768]{0,1:T(8,128)(2,1)} async-done(((bf16[1024,768]{0,1:T(8,128)(2,1)}), bf16[2048,768]{0,1:T(8,128)(2,1)}) %all-gather.14.cloned.1.call-update) | async-done | bytes 3145744 | tf_op jit(solution)/shard_map/all_gather | solution.py:39
  1011.8 7.2 fusion.48
  1019.4 8.0 convolution_convert_fusion
  1027.3 4.6 convolution_convert_fusion.2
  1031.9 4.6 convolution_convert_fusion.1
  1039.6 4.2 convolution_convert_fusion.3
  1043.9 196.1 %all-reduce.12.cloned.1.call-done = (f32[2048,768]{1,0:T(8,128)}, f32[2048,768]{1,0:T(8,128)}) async-done(((f32[2048,768]{1,0:T(8,128)}, f32[2048,768]{1,0:T(8,128)}), (f32[2048,768]{1,0:T(8,128)}, f32[2048,768]{1,0:T(8,128)})) %all-reduce.12.cloned.1.call-update) | async-done | bytes 12582928 | tf_op jit(solution)/shard_map/psum | solution.py:35
  1239.9 4.9 fusion.15
  1244.8 12.2 all-reduce.1
  1258.2 5.2 psum.112
  1263.4 7.1 add_convert_fusion
  1273.8 3.2 fusion.11
  1277.0 196.2 %all-reduce.14.cloned.1.call-done = (bf16[768,768]{1,0:T(8,128)(2,1)}, bf16[384,768]{1,0:T(8,128)(2,1)}, bf16[768,1024]{1,0:T(8,128)(2,1)}, bf16[768,1024]{1,0:T(8,128)(2,1)}, bf16[1024,768]{1,0:T(8,128)(2,1)}) async-done(((bf16[768,768]{1,0:T(8,128)(2,1)}, bf16[384,768]{1,0:T(8,128)(2,1)}, bf16[768,1024]{1,0:T(8,128)(2,1)}, bf16[768,1024]{1,0:T(8,128)(2,1)}, bf16[1024,768]{1,0:T(8,128)(2,1)}), ...) | async-done | bytes 6488080 | tf_op jit(solution)/shard_map/psum | solution.py:174
  1473.3 3.0 convert_element_type.146
  (153 shorter events, 48.0 us)
Async XLA Ops:
  7.2 295.9 %copy-start = (bf16[768,1024]{1,0:T(8,128)(2,1)S(1)}, bf16[768,1024]{1,0:T(8,128)(2,1)}, u32[]{:S(2)}) copy-start(bf16[768,1024]{1,0:T(8,128)(2,1)} %param.16) | copy-start | bytes 4718596
  7.2 95.4 %reduce-scatter.6.cloned.1.call-start = ((), (), s32[]{:S(2)}) async-start(), calls=%async_computation.5 | async-start | bytes 9437184 | tf_op jit(solution)/shard_map/reduce_scatter | solution.py:43
  23.5 130.5 %all-gather.6.cloned.1.call-start = ((), (), s32[]{:S(2)}) async-start(), calls=%async_computation.6 | async-start | bytes 2359296 | tf_op jit(solution)/shard_map/all_gather | solution.py:39
  24.3 93.4 %copy-start.18 = (pred[512,512]{0,1:T(8,128)(4,1)}, pred[512,512]{0,1:T(8,128)(4,1)S(1)}, u32[]{:S(2)}) copy-start(pred[512,512]{0,1:T(8,128)(4,1)S(1)} %iota_compare_fusion) | copy-start | bytes 786436
  111.7 3.6 slice-start.4
  113.2 6.3 copy-start.24
  117.6 3.3 copy-start.6
  126.7 153.1 %all-reduce.8.cloned.1.call-start = ((), (), s32[]{:S(2)}) async-start(), calls=%async_computation.7 | async-start | bytes 12582912 | tf_op jit(solution)/shard_map/psum | solution.py:35
  160.1 221.6 %reduce-scatter.12.cloned.1.call-start = ((), (), s32[]{:S(2)}) async-start(), calls=%async_computation.11 | async-start | bytes 12582912 | tf_op jit(solution)/shard_map/reduce_scatter | solution.py:121
  169.3 122.9 %copy-start.25 = (f32[768]{0:T(1024)S(1)}, f32[768]{0:T(1024)}, u32[]{:S(2)}) copy-start(f32[768]{0:T(1024)} %param.15) | copy-start | bytes 9220
  169.3 313.9 %reduce-scatter.10.cloned.1.call-start = ((), (), s32[]{:S(2)}) async-start(), calls=%async_computation.9 | async-start | bytes 12582912 | tf_op jit(solution)/shard_map/reduce_scatter | solution.py:112
  292.2 5.2 copy-start.33
  303.0 281.6 %reduce-scatter.8.cloned.1.call-start = ((), (), s32[]{:S(2)}) async-start(), calls=%async_computation.8 | async-start | bytes 12582912 | tf_op jit(solution)/shard_map/reduce_scatter | solution.py:111
  310.7 339.0 %all-gather.10.cloned.1.call-start = ((), (), s32[]{:S(2)}) async-start(), calls=%async_computation.12 | async-start | bytes 6291456 | tf_op jit(solution)/shard_map/all_gather | solution.py:124
  592.8 115.8 %all-gather.12.cloned.1.call-start = ((), (), s32[]{:S(2)}) async-start(), calls=%async_computation.13 | async-start | bytes 6291456 | tf_op jit(solution)/shard_map/all_gather | solution.py:125
  593.6 245.4 %all-reduce.10.cloned.1.call-start = ((), (), s32[]{:S(2)}) async-start(), calls=%async_computation.14 | async-start | bytes 12582912 | tf_op jit(solution)/shard_map/psum | solution.py:35
  719.2 186.8 %reduce-scatter.14.cloned.1.call-start = ((), (), s32[]{:S(2)}) async-start(), calls=%async_computation.15 | async-start | bytes 4718592 | tf_op jit(solution)/shard_map/reduce_scatter | solution.py:43
  849.4 9.3 copy-start.10
  856.1 2.6 copy-start.2
  862.2 102.7 %all-gather.8.cloned.1.call-start = ((), (), s32[]{:S(2)}) async-start(), calls=%async_computation.10 | async-start | bytes 6291456 | tf_op jit(solution)/shard_map/all_gather | solution.py:115
  863.0 148.8 %all-gather.14.cloned.1.call-start = ((), (), s32[]{:S(2)}) async-start(), calls=%async_computation.16 | async-start | bytes 4718592 | tf_op jit(solution)/shard_map/all_gather | solution.py:39
  909.8 5.4 copy-start.15
  909.8 5.4 copy-start.17
  915.2 3.0 slice-start.5
  916.8 3.2 slice-start.6
  916.8 3.2 copy-start.19
  916.9 3.2 copy-start.28
  922.5 42.4 %copy-start.34 = (bf16[1024,768]{1,0:T(8,128)(2,1)S(1)}, bf16[1024,768]{1,0:T(8,128)(2,1)}, u32[]{:S(2)}) copy-start(bf16[1024,768]{1,0:T(8,128)(2,1)} %param.18) | copy-start | bytes 4718596
  925.8 86.1 %copy-start.35 = (bf16[768,768]{1,0:T(8,128)(2,1)S(1)}, bf16[768,768]{1,0:T(8,128)(2,1)}, u32[]{:S(2)}) copy-start(bf16[768,768]{1,0:T(8,128)(2,1)} %param.13) | copy-start | bytes 3538948
  925.8 314.2 %all-reduce.12.cloned.1.call-start = ((), (), s32[]{:S(2)}) async-start(), calls=%async_computation.17 | async-start | bytes 25165824 | tf_op jit(solution)/shard_map/psum | solution.py:35
  1019.1 454.2 %all-reduce.14.cloned.1.call-start = ((), (), s32[]{:S(2)}) async-start(), calls=%async_computation.18 | async-start | bytes 12976128 | tf_op jit(solution)/shard_map/psum | solution.py:174
  1019.3 8.0 copy-start.8
  1019.4 8.0 copy-start.30
  1027.3 4.6 copy-start.31
  1027.3 9.1 slice-start
  1031.9 4.6 slice-start.1
  1031.9 4.6 copy-start.9
  1036.5 2.3 copy-start.3
  1036.5 2.3 copy-start.26
  1036.5 3.1 copy-start.32
  1263.4 7.1 slice-start.2
  1263.4 7.1 slice-start.3
  1263.4 8.5 copy-start.4
  1263.4 10.4 copy-start.5
  1473.3 5.2 copy-start.13
  1473.3 7.2 copy-start.12
  1478.4 4.1 copy-start.11
  1480.5 4.0 copy-start.1
  (9 other events, 13.6 us)
Sparse Core Ops, SparseCore 0:
  23.6 78.9 reduce-scatter.5
  126.8 27.1 all-gather.5
  160.2 119.5 all-reduce.7
  282.0 99.6 reduce-scatter.11
  383.8 99.3 reduce-scatter.9
  485.3 99.2 reduce-scatter.7
  593.0 56.7 all-gather.9
  651.9 56.7 all-gather.11
  719.4 119.5 all-reduce.9
  862.4 43.6 reduce-scatter.13
  908.1 56.7 all-gather.7
  966.9 44.8 all-gather.13
  1019.2 220.6 all-reduce.11
  1243.7 229.5 all-reduce.13
where the time goes:
time: 1490 us
  waiting for transfers between devices  1230 us (83%)
  matrix products  112 us (8%)
  other arithmetic  66.5 us (4%)
  blocking collectives  33.5 us (2%)
  local copies, waits for them, and re-layouts  33.1 us (2%)
    psum x3, waiting for transfers between devices, width_total(): return lax.psum(values, 'col')  426 us
    psum x1, waiting for transfers between devices, body(): lax.psum(w_qkv_grad.astype(jnp.bfloat16), 'dp').astype(jnp.float32)  196 us
    reduce_scatter x2, waiting for transfers between devices, split_rows(): lax.psum_scatter(lax.dot_general(left, right, (((1,), (contract,)), ((),...  120 us
    reduce_scatter x1, waiting for transfers between devices, body(): lax.psum_scatter(up_part, 'row', scatter_dimension=0, tiled=True)  102 us
    reduce_scatter x1, waiting for transfers between devices, body(): lax.psum_scatter(gate_part, 'row', scatter_dimension=0, tiled=True)  101 us
    reduce_scatter x1, waiting for transfers between devices, body(): lax.psum_scatter(act_grad_part, 'row', scatter_dimension=0, tiled=True)  70.9 us
    all_gather x2, waiting for transfers between devices, join_rows(): return lax.all_gather(values, 'row', axis=0, tiled=True)  65.8 us
    all_gather x1, waiting for transfers between devices, body(): lax.all_gather(gate_half, 'row', axis=0, tiled=True)  55.6 us
  transfers between devices with their start and end apart: 14, of which 14 were waited for; matrix products, arithmetic and copies ran while one was open for 7% of the time, Pallas kernels for 0%

commit v1 on v0

--- a/solution.py
+++ b/solution.py
@@ -12,6 +12,11 @@
 THETA = 100000.0
 
 
+def add_all(shard, axis):
+    shards = lax.all_gather(shard, axis)
+    return jnp.sum(shards, axis=0)
+
+
 def rotate(values, cosine, sine, sign):
     half = values.shape[-1] // 2
     first = values[..., :half]
@@ -32,7 +37,7 @@
 
 
 def width_total(values):
-    return lax.psum(values, "col")
+    return add_all(values, "col")
 
 
 def join_rows(values):

time: 1490 us -> 1700 us (1.14)
  waiting for transfers between devices: 1230 us -> 1370 us
  other arithmetic: 66.5 us -> 126 us
    all_gather x0 -> x4, waiting for transfers between devices: none -> 562 us  [add_all(): shards = lax.all_gather(shard, axis)]
    psum x3 -> x0, waiting for transfers between devices: 426 us -> none  [width_total(): return lax.psum(values, 'col')]
    reduce_sum x0 -> x4, other arithmetic: none -> 53.6 us  [add_all(): return jnp.sum(shards, axis=0)]
    psum x1, waiting for transfers between devices: 196 us -> 221 us  [body(): lax.psum(w_qkv_grad.astype(jnp.bfloat16), 'dp').astype(jnp.float32)]
  transfers between devices with their start and end apart: 14 -> 15, of which waited for: 14 -> 15; matrix products, arithmetic and copies ran while one was open for 7% -> 8% of each run, Pallas kernels for 0% -> 0%
where the time goes in v1:
time: 1700 us
  waiting for transfers between devices  1370 us (81%)
  other arithmetic  126 us (7%)
  matrix products  121 us (7%)
  blocking collectives  32.8 us (2%)
  local copies, waits for them, and re-layouts  27.7 us (2%)
    all_gather x4, waiting for transfers between devices, add_all(): shards = lax.all_gather(shard, axis)  562 us
    psum x1, waiting for transfers between devices, body(): lax.psum(w_qkv_grad.astype(jnp.bfloat16), 'dp').astype(jnp.float32)  221 us
    reduce_scatter x2, waiting for transfers between devices, split_rows(): lax.psum_scatter(lax.dot_general(left, right, (((1,), (contract,)), ((),...  121 us
    reduce_scatter x1, waiting for transfers between devices, body(): lax.psum_scatter(gate_part, 'row', scatter_dimension=0, tiled=True)  102 us
    reduce_scatter x1, waiting for transfers between devices, body(): lax.psum_scatter(up_part, 'row', scatter_dimension=0, tiled=True)  102 us
    reduce_scatter x1, waiting for transfers between devices, body(): lax.psum_scatter(act_grad_part, 'row', scatter_dimension=0, tiled=True)  57 us
    all_gather x1, waiting for transfers between devices, body(): lax.all_gather(gate_half, 'row', axis=0, tiled=True)  55.3 us
    reduce_sum x4, other arithmetic, add_all(): return jnp.sum(shards, axis=0)  53.6 us
  transfers between devices with their start and end apart: 15, of which 15 were waited for; matrix products, arithmetic and copies ran while one was open for 8% of the time, Pallas kernels for 0%

profile of v1, /device:TPU:0, one launch (start us, length us, event | category | flops | bytes accessed | tf_op | source)
XLA Modules:
  0.0 1696.0 jit_solution(13305660452156233386)
XLA Ops:
  9.9 5.9 psum.77
  16.5 7.6 fusion.30
  25.6 77.5 %reduce-scatter.6.cloned.1.call-done = f32[1024,768]{1,0:T(8,128)} async-done(((f32[2048,768]{1,0:T(8,128)}), f32[1024,768]{1,0:T(8,128)}) %reduce-scatter.6.cloned.1.call-update) | async-done | bytes 3145744 | tf_op jit(solution)/shard_map/reduce_scatter | solution.py:48
  103.2 3.5 copy.27
  106.7 5.6 reshape.64
  127.0 27.0 %all-gather.14.cloned.1.call-done = bf16[2048,384]{0,1:T(8,128)(2,1)} async-done(((bf16[1024,384]{0,1:T(8,128)(2,1)}), bf16[2048,384]{0,1:T(8,128)(2,1)}) %all-gather.14.cloned.1.call-update) | async-done | bytes 1572880 | tf_op jit(solution)/shard_map/all_gather | solution.py:44
  154.0 6.0 fusion.42
  160.1 11.0 fusion.46
  171.1 143.8 %all-gather.24.cloned.1.call-done = f32[8192,768]{1,0:T(8,128)} async-done(((f32[2048,768]{1,0:T(8,128)}), f32[8192,768]{1,0:T(8,128)}) %all-gather.24.cloned.1.call-update) | async-done | bytes 25165840 | tf_op jit(solution)/shard_map/all_gather | solution.py:16
  315.0 13.3 reduce_sum.110
  328.3 7.2 multiply_reduce_fusion.2
  335.4 5.3 psum.78
  345.9 5.6 fusion.44
  351.6 7.6 fusion.43
  359.7 57.0 %reduce-scatter.12.cloned.1.call-done = f32[1024,1024]{1,0:T(8,128)} async-done(((f32[2048,1024]{1,0:T(8,128)}), f32[1024,1024]{1,0:T(8,128)}) %reduce-scatter.12.cloned.1.call-update) | async-done | bytes 4194320 | tf_op jit(solution)/shard_map/reduce_scatter | solution.py:126
  416.7 101.5 %reduce-scatter.10.cloned.1.call-done = f32[1024,1024]{1,0:T(8,128)} async-done(((f32[2048,1024]{1,0:T(8,128)}), f32[1024,1024]{1,0:T(8,128)}) %reduce-scatter.10.cloned.1.call-update) | async-done | bytes 4194320 | tf_op jit(solution)/shard_map/reduce_scatter | solution.py:117
  518.2 101.5 %reduce-scatter.8.cloned.1.call-done = f32[1024,1024]{1,0:T(8,128)} async-done(((f32[2048,1024]{1,0:T(8,128)}), f32[1024,1024]{1,0:T(8,128)}) %reduce-scatter.8.cloned.1.call-update) | async-done | bytes 4194320 | tf_op jit(solution)/shard_map/reduce_scatter | solution.py:116
  619.7 8.1 multiply_convert_fusion.1
  629.4 55.3 %all-gather.18.cloned.1.call-done = bf16[2048,1024]{1,0:T(8,128)(2,1)} async-done(((bf16[1024,1024]{1,0:T(8,128)(2,1)}), bf16[2048,1024]{1,0:T(8,128)(2,1)}) %all-gather.18.cloned.1.call-update) | async-done | bytes 4194320 | tf_op jit(solution)/shard_map/all_gather | solution.py:129
  684.7 8.3 fusion.47
  693.1 50.5 %all-gather.20.cloned.1.call-done = bf16[2048,1024]{1,0:T(8,128)(2,1)} async-done(((bf16[1024,1024]{1,0:T(8,128)(2,1)}), bf16[2048,1024]{1,0:T(8,128)(2,1)}) %all-gather.20.cloned.1.call-update) | async-done | bytes 4194320 | tf_op jit(solution)/shard_map/all_gather | solution.py:130
  743.6 11.0 convolution_add_fusion
  754.9 47.6 %all-gather.16.cloned.1.call-done = bf16[2048,1024]{1,0:T(8,128)(2,1)} async-done(((bf16[1024,1024]{1,0:T(8,128)(2,1)}), bf16[2048,1024]{1,0:T(8,128)(2,1)}) %all-gather.16.cloned.1.call-update) | async-done | bytes 4194320 | tf_op jit(solution)/shard_map/all_gather | solution.py:120
  802.5 8.7 fusion.45
  811.3 147.5 %all-gather.28.cloned.1.call-done = f32[8192,768]{1,0:T(8,128)} async-done(((f32[2048,768]{1,0:T(8,128)}), f32[8192,768]{1,0:T(8,128)}) %all-gather.28.cloned.1.call-update) | async-done | bytes 25165840 | tf_op jit(solution)/shard_map/all_gather | solution.py:16
  958.7 14.9 reduce_sum.113
  973.6 8.7 multiply_reduce_fusion
  982.3 5.0 psum.79
  987.3 127.9 %all-gather.26.cloned.1.call-done = f32[8192,768]{1,0:T(8,128)} async-done(((f32[2048,768]{1,0:T(8,128)}), f32[8192,768]{1,0:T(8,128)}) %all-gather.26.cloned.1.call-update) | async-done | bytes 25165840 | tf_op jit(solution)/shard_map/all_gather | solution.py:16
  1115.1 12.7 reduce_sum.112
  1127.8 10.2 multiply_add_fusion
  1140.7 3.5 fusion.19
  1144.6 43.3 %reduce-scatter.14.cloned.1.call-done = f32[1024,384]{1,0:T(8,128)} async-done(((f32[2048,384]{1,0:T(8,128)}), f32[1024,384]{1,0:T(8,128)}) %reduce-scatter.14.cloned.1.call-update) | async-done | bytes 1572880 | tf_op jit(solution)/shard_map/reduce_scatter | solution.py:48
  1191.7 5.6 fusion.28
  1197.4 5.2 fusion.1
  1209.0 8.0 convolution_convert_fusion
  1217.0 4.6 convolution_convert_fusion.2
  1221.6 4.6 convolution_convert_fusion.1
  1228.4 25.3 %all-gather.22.cloned.1.call-done = bf16[2048,768]{0,1:T(8,128)(2,1)} async-done(((bf16[1024,768]{0,1:T(8,128)(2,1)}), bf16[2048,768]{0,1:T(8,128)(2,1)}) %all-gather.22.cloned.1.call-update) | async-done | bytes 3145744 | tf_op jit(solution)/shard_map/all_gather | solution.py:44
  1253.8 6.9 convolution_convert_fusion.3
  1261.9 7.3 fusion.48
  1269.3 220.8 %all-reduce.4.cloned.1.call-done = (bf16[768,768]{1,0:T(8,128)(2,1)}, bf16[384,768]{1,0:T(8,128)(2,1)}, bf16[768,1024]{1,0:T(8,128)(2,1)}, bf16[768,1024]{1,0:T(8,128)(2,1)}, bf16[1024,768]{1,0:T(8,128)(2,1)}) async-done(((bf16[768,768]{1,0:T(8,128)(2,1)}, bf16[384,768]{1,0:T(8,128)(2,1)}, bf16[768,1024]{1,0:T(8,128)(2,1)}, bf16[768,1024]{1,0:T(8,128)(2,1)}, bf16[1024,768]{1,0:T(8,128)(2,1)}), ...) | async-done | bytes 6488080 | tf_op jit(solution)/shard_map/psum | solution.py:179
  1501.9 143.3 %all-gather.30.cloned.1.call-done = f32[8192,768]{1,0:T(8,128)} async-done(((f32[2048,768]{1,0:T(8,128)}), f32[8192,768]{1,0:T(8,128)}) %all-gather.30.cloned.1.call-update) | async-done | bytes 25165840 | tf_op jit(solution)/shard_map/all_gather | solution.py:16
  1645.2 12.7 reduce_sum.116
  1657.9 4.9 fusion.15
  1662.8 11.7 all-reduce
  1675.7 5.0 psum.80
  1680.7 8.3 fusion.11
  (145 shorter events, 56.8 us)
Async XLA Ops:
  7.2 344.4 %copy-start = (bf16[768,1024]{1,0:T(8,128)(2,1)S(1)}, bf16[768,1024]{1,0:T(8,128)(2,1)}, u32[]{:S(2)}) copy-start(bf16[768,1024]{1,0:T(8,128)(2,1)} %param.16) | copy-start | bytes 4718596
  7.2 96.0 %reduce-scatter.6.cloned.1.call-start = ((), (), s32[]{:S(2)}) async-start(), calls=%async_computation.5 | async-start | bytes 9437184 | tf_op jit(solution)/shard_map/reduce_scatter | solution.py:48
  24.1 129.9 %all-gather.14.cloned.1.call-start = ((), (), s32[]{:S(2)}) async-start(), calls=%async_computation.6 | async-start | bytes 2359296 | tf_op jit(solution)/shard_map/all_gather | solution.py:44
  24.9 93.4 %copy-start.15 = (pred[512,512]{0,1:T(8,128)(4,1)}, pred[512,512]{0,1:T(8,128)(4,1)S(1)}, u32[]{:S(2)}) copy-start(pred[512,512]{0,1:T(8,128)(4,1)S(1)} %iota_compare_fusion) | copy-start | bytes 786436
  112.3 3.6 slice-start.2
  113.8 6.3 copy-start.21
  116.2 2.0 copy-start.17
  116.2 2.0 copy-start.19
  116.5 1.7 copy-start.11
  116.5 1.7 copy-start.13
  118.2 3.3 copy-start.3
  126.7 188.3 %all-gather.24.cloned.1.call-start = ((), (), s32[]{:S(2)}) async-start(), calls=%async_computation.15 | async-start | bytes 31457280 | tf_op jit(solution)/shard_map/all_gather | solution.py:16
  160.0 256.6 %reduce-scatter.12.cloned.1.call-start = ((), (), s32[]{:S(2)}) async-start(), calls=%async_computation.10 | async-start | bytes 12582912 | tf_op jit(solution)/shard_map/reduce_scatter | solution.py:126
  171.1 347.1 %reduce-scatter.10.cloned.1.call-start = ((), (), s32[]{:S(2)}) async-start(), calls=%async_computation.8 | async-start | bytes 12582912 | tf_op jit(solution)/shard_map/reduce_scatter | solution.py:117
  328.3 12.4 copy-start.25
  340.7 5.2 copy-start.31
  344.2 1.7 copy-start.4
  351.5 268.2 %reduce-scatter.8.cloned.1.call-start = ((), (), s32[]{:S(2)}) async-start(), calls=%async_computation.7 | async-start | bytes 12582912 | tf_op jit(solution)/shard_map/reduce_scatter | solution.py:116
  359.2 325.6 %all-gather.18.cloned.1.call-start = ((), (), s32[]{:S(2)}) async-start(), calls=%async_computation.11 | async-start | bytes 6291456 | tf_op jit(solution)/shard_map/all_gather | solution.py:129
  627.8 115.8 %all-gather.20.cloned.1.call-start = ((), (), s32[]{:S(2)}) async-start(), calls=%async_computation.12 | async-start | bytes 6291456 | tf_op jit(solution)/shard_map/all_gather | solution.py:130
  628.6 173.9 %all-gather.16.cloned.1.call-start = ((), (), s32[]{:S(2)}) async-start(), calls=%async_computation.9 | async-start | bytes 6291456 | tf_op jit(solution)/shard_map/all_gather | solution.py:120
  629.3 329.4 %all-gather.28.cloned.1.call-start = ((), (), s32[]{:S(2)}) async-start(), calls=%async_computation.17 | async-start | bytes 31457280 | tf_op jit(solution)/shard_map/all_gather | solution.py:16
  754.6 47.9 %copy-start.32 = (bf16[1024,768]{1,0:T(8,128)(2,1)S(1)}, bf16[1024,768]{1,0:T(8,128)(2,1)}, u32[]{:S(2)}) copy-start(bf16[1024,768]{1,0:T(8,128)(2,1)} %param.18) | copy-start | bytes 4718596
  754.6 360.5 %all-gather.26.cloned.1.call-start = ((), (), s32[]{:S(2)}) async-start(), calls=%async_computation.16 | async-start | bytes 31457280 | tf_op jit(solution)/shard_map/all_gather | solution.py:16
  811.2 376.6 %reduce-scatter.14.cloned.1.call-start = ((), (), s32[]{:S(2)}) async-start(), calls=%async_computation.13 | async-start | bytes 4718592 | tf_op jit(solution)/shard_map/reduce_scatter | solution.py:48
  1127.8 12.9 copy-start.7
  1138.0 2.7 copy-start.2
  1144.3 47.4 %copy-start.16 = (pred[512,512]{0,1:T(8,128)(4,1)S(1)}, pred[512,512]{0,1:T(8,128)(4,1)}, u32[]{:S(2)}) copy-start(pred[512,512]{0,1:T(8,128)(4,1)} %copy-done.15) | copy-start | bytes 786436
  1144.3 109.5 %all-gather.22.cloned.1.call-start = ((), (), s32[]{:S(2)}) async-start(), calls=%async_computation.14 | async-start | bytes 4718592 | tf_op jit(solution)/shard_map/all_gather | solution.py:44
  1191.7 5.7 copy-start.22
  1197.3 5.2 copy-start.12
  1197.4 5.2 copy-start.14
  1202.6 1.4 copy-start.18
  1208.7 281.4 %all-reduce.4.cloned.1.call-start = ((), (), s32[]{:S(2)}) async-start(), calls=%async_computation.19 | async-start | bytes 12976128 | tf_op jit(solution)/shard_map/psum | solution.py:179
  1209.0 8.0 copy-start.5
  1209.0 8.0 copy-start.29
  1217.0 4.6 copy-start.30
  1217.0 9.1 slice-start
  1221.6 4.6 slice-start.1
  1221.6 4.6 copy-start.6
  1226.1 27.6 %copy-start.24 = (f32[2048,1]{0,1:T(1,128)S(1)}, f32[2048,1]{0,1:T(1,128)}, u32[]{:S(2)}) copy-start(f32[2048,1]{0,1:T(1,128)} %copy-done.23) | copy-start | bytes 24580
  1226.1 27.6 %copy-start.26 = (f32[768]{0:T(1024)S(1)}, f32[768]{0:T(1024)}, u32[]{:S(2)}) copy-start(f32[768]{0:T(1024)} %param.12) | copy-start | bytes 9220
  1260.7 384.5 %all-gather.30.cloned.1.call-start = ((), (), s32[]{:S(2)}) async-start(), calls=%async_computation.18 | async-start | bytes 31457280 | tf_op jit(solution)/shard_map/all_gather | solution.py:16
  1490.1 5.2 copy-start.10
  1490.1 7.3 copy-start.9
  1495.3 4.5 copy-start.8
  1657.9 4.9 copy-start.27
  1680.7 8.3 copy-start.1
  (4 other events, 4.0 us)
Sparse Core Ops, SparseCore 0:
  24.2 78.9 reduce-scatter.5
  126.8 27.1 all-gather.13
  160.2 154.7 all-gather.23
  317.1 99.4 reduce-scatter.11
  418.8 99.3 reduce-scatter.9
  520.3 99.3 reduce-scatter.7
  628.0 56.7 all-gather.17
  686.8 56.7 all-gather.19
  745.7 56.7 all-gather.15
  803.9 154.7 all-gather.27
  960.3 154.7 all-gather.25
  1144.4 43.3 reduce-scatter.13
  1208.8 44.9 all-gather.21
  1260.8 229.2 all-reduce.3
  1491.5 153.6 all-gather.29
